TPU v7x, 512 devices: a 4x2x32 block of a 4x8x32 slice. The times are simulated.
512 devices in a mesh: rep: 2 (over y), seq: 32 (over z), tp: 8 (over x, core).
Axes of the slice: x: 4, y: 2, z: 32, core: 2. Of those that a mesh axis runs over, the one named last changes fastest.
The devices are a block of a 4x8x32 slice.
Arguments:
- queries: bfloat16 [128, 64, 128], P(('rep', 'seq')), parts along dimension 0, may hold values from -9 to 9
- key_pages: bfloat16 [8192, 8, 64, 128], P(('rep', 'seq'), 'tp'), parts along dimension 0, may hold values from -4 to 4
- value_pages: bfloat16 [8192, 8, 64, 128], P(('rep', 'seq'), 'tp'), parts along dimension 0, may hold values from -6 to 6
- page_owner: int32 [128, 1024], P('rep'), parts along dimension 0, may hold values from 0 to 31, as said below
- page_local: int32 [128, 1024], P('rep'), parts along dimension 0, may hold values from 0 to 127, as said below
- seq_lengths: int32 [128], P('rep'), parts along dimension 0, may hold values from 1 to 65536, as said below
Outputs:
- attention: bfloat16 [128, 64, 128], P(('rep', 'seq'), 'tp'), parts along dimension 0
There are 2 independent parts, one for each index of `rep`. A program takes and returns all parts, laid end to end along the dimension named above; each array names one. Nothing has to cross between parts.
Inputs may be any that keep to these rules, and one draw needn't show every extreme that they name: The live slots (s * 64 < seq_lengths[b]) name pairs (page_owner, page_local) that are all different; the other slots hold 0. `page_local`: see page_owner. `seq_lengths`: one sequence has exactly 65536 tokens; the live slots of all sequences together number at most half of the 4096 pages.
All inputs are finite; a program needn't handle non-finite values.
Results may differ from a plain program's by a relative error of at most 0.008.
Values may be sent and summed in bfloat16 or wider, within the bound.
A program may use at most 64 MiB of HBM per device.

v0:
```python
import math

import jax
import jax.numpy as jnp
from jax import lax
from jax.sharding import PartitionSpec as P

HQ = 64
KVH = 8


score_shift = 8.0


def copy_for_each(value, axis):
    devices = lax.axis_size(axis)
    return lax.all_to_all(
        jnp.broadcast_to(value[None], (devices, *value.shape)), axis, 0, 0, tiled=True
    )


def laid_out(pieces, dim):
    shape = list(pieces.shape[1:])
    shape[dim] *= pieces.shape[0]
    return jnp.moveaxis(pieces, 0, dim).reshape(shape)


def gathered_copies(value, axis, dim):
    pieces = copy_for_each(value, axis)
    return laid_out(pieces, dim)


def split_up(value, dim, devices):
    before, after = (value.shape[:dim], value.shape[dim + 1 :])
    return jnp.moveaxis(value.reshape(*before, devices, -1, *after), dim, 0)


def summed_on_arrival(value, axis, dim):
    devices = lax.axis_size(axis)
    pieces = lax.all_to_all(split_up(value, dim, devices), axis, 0, 0, tiled=True)
    return jnp.sum(pieces.astype(jnp.float32), axis=0)


def sent_together(arrays, axis, dim, along):
    ends, at = ([], 0)
    for a in arrays[:-1]:
        at += a.shape[along]
        ends.append(at)
    both = jnp.concatenate(arrays, axis=along)
    return tuple(jnp.split(summed_on_arrival(both, axis, dim), ends, axis=along))


def body(queries, key_pages, value_pages, page_owner, page_local, seq_lengths):
    seq_count = page_owner.shape[0]
    slot_count = page_owner.shape[1]
    pool_pages = key_pages.shape[0]
    kv_local = key_pages.shape[1]
    page_len = key_pages.shape[2]
    head_dim = key_pages.shape[3]
    group_size = HQ // KVH
    heads_local = kv_local * group_size
    seq_rank = lax.axis_index("seq")
    tp_rank = lax.axis_index("tp")
    slot_ids = jnp.arange(slot_count, dtype=jnp.int32)
    slot_fill = jnp.clip(seq_lengths[:, None] - slot_ids[None, :] * page_len, 0, page_len)
    owned = (slot_fill > 0) & (page_owner == seq_rank)
    pool_range = jnp.arange(pool_pages, dtype=jnp.int32)
    matches = ((page_local[:, :, None] == pool_range[None, None, :]) & owned[:, :, None]).astype(
        jnp.bfloat16
    )
    fill_weight = slot_fill.astype(jnp.bfloat16)
    fill_table = jnp.einsum("bsp,bs->bp", matches, fill_weight, preferred_element_type=jnp.float32)
    hit_table = jnp.sum(matches.astype(jnp.float32), axis=1)
    seq_weight = jnp.arange(seq_count, dtype=jnp.float32)
    page_seq = jnp.dot(seq_weight, hit_table, precision=lax.Precision.HIGHEST).astype(jnp.int32)
    page_fill = jnp.sum(fill_table, axis=0).astype(jnp.int32)
    local_heads = lax.dynamic_slice_in_dim(queries, tp_rank * heads_local, heads_local, 1)
    head_queries = gathered_copies(local_heads, "seq", 0)
    query_flat = head_queries.reshape(seq_count, heads_local * head_dim)
    score_scale = 1.0 / math.sqrt(head_dim)
    seq_range = jnp.arange(seq_count, dtype=jnp.int32)
    count = page_seq.shape[0]
    selector = page_seq[:, None] == seq_range[None, :]
    picked = jnp.dot(
        selector.astype(jnp.bfloat16), query_flat, preferred_element_type=jnp.float32
    ).astype(jnp.bfloat16)
    picked = picked.reshape(count, kv_local, group_size, head_dim)
    scores = (
        jnp.einsum("pkgd,pktd->pkgt", picked, key_pages, preferred_element_type=jnp.float32)
        * score_scale
    )
    live_mask = jnp.arange(page_len, dtype=jnp.int32)[None, :] < page_fill[:, None]
    weight = jnp.where(live_mask[:, None, None, :], jnp.exp(scores - score_shift), 0.0)
    page_total = jnp.sum(weight, axis=-1)
    page_sum = jnp.einsum(
        "pkgt,pktd->pkgd",
        weight.astype(jnp.bfloat16),
        value_pages,
        preferred_element_type=jnp.float32,
    )
    spread = selector.astype(jnp.float32).T
    numerator = jnp.dot(
        spread, page_sum.reshape(count, heads_local * head_dim), precision=lax.Precision.HIGHEST
    )
    denominator = jnp.dot(
        spread, page_total.reshape(count, heads_local), precision=lax.Precision.HIGHEST
    )
    numerator, denominator = (numerator, denominator)
    own_rows = seq_count // lax.axis_size("seq")
    summed_num, summed_den = sent_together(
        (numerator.astype(jnp.bfloat16), denominator.astype(jnp.bfloat16)), "seq", 0, 1
    )
    result = summed_num.reshape(own_rows, heads_local, head_dim) / summed_den[..., None]
    return result.astype(jnp.bfloat16)


def solution(mesh):
    placed = (
        P(("rep", "seq"), None, None),
        P(("rep", "seq"), "tp", None, None),
        P(("rep", "seq"), "tp", None, None),
        P("rep", None),
        P("rep", None),
        P("rep"),
    )
    return jax.shard_map(
        body, mesh=mesh, in_specs=placed, out_specs=P(("rep", "seq"), "tp", None), check_vma=False
    )
```

profile of v0, /device:TPU:46, one launch (start us, length us, event | category | flops | bytes accessed | tf_op | source)
XLA Modules:
  0.0 171.1 jit_solution(13571377275870604458)
XLA Ops:
  0.0 0.0 copy-start
  0.0 0.8 constant_dynamic-slice_fusion
  0.8 0.7 broadcast_in_dim.11
  1.5 45.8 %all-to-all-start = ((bf16[32,2,8,128]{3,2,1,0:T(8,128)(2,1)}), bf16[32,2,8,128]{3,2,1,0:T(8,128)(2,1)S(1)}, u32[]{:S(2)}, u32[]{:S(2)}) async-start(bf16[32,2,8,128]{3,2,1,0:T(8,128)(2,1)} %broadcast_in_dim.11), calls=%async_computation | async-start | bytes 262144 | tf_op jit(solution)/shard_map/all_to_all | solution.py:17
  47.3 0.8 fusion.37
  48.1 1.1 fusion.36
  49.2 0.0 copy-start.1
  49.2 42.6 %fusion.26 = s32[128]{0:T(128)S(1)} fusion(s32[64,1024]{1,0:T(8,128)} %param.10, pred[64,1024]{1,0:T(8,128)(4,1)S(1)} %fusion.36, bf16[64,1024,1]{1,0,2:T(8,128)(2,1)S(1)} %fusion.37), kind=kOutput, calls=%fused_computation.20 | convolution fusion | flops 33554560 | bytes 459264 | tf_op jit(solution)/shard_map/bsp,bs->bp/dot_general | solution.py:72
  91.8 0.1 iota_compare_fusion.1
  91.9 0.0 copy-done.1
  91.9 19.9 %convert_reduce_fusion = f32[64,128]{1,0:T(8,128)S(1)} fusion(s32[64,1024]{1,0:T(8,128)S(1)} %copy-done.1, pred[64,1024]{1,0:T(8,128)(4,1)S(1)} %fusion.36), kind=kLoop, calls=%fused_computation | loop fusion | flops 41934848 | bytes 360448 | tf_op jit(solution)/shard_map/reduce_sum | solution.py:73
  111.8 0.1 fusion.29
  112.0 0.0 all-to-all-done
  112.0 0.3 fusion.22
  112.3 2.9 %fusion.45 = (f32[128,8]{1,0:T(8,128)S(1)}, bf16[128,8,64]{2,1,0:T(8,128)(2,1)S(1)}) fusion(bf16[128,8,128]{2,1,0:T(8,128)(2,1)S(1)} %bitcast.50, bf16[128,1,64,128]{3,2,1,0:T(8,128)(2,1)} %param.7, pred[128,64]{1,0:T(8,128)(4,1)S(1)} %iota_compare_fusion.1), kind=kOutput, calls=%fused_computation.47 | convolution fusion | flops 17103872 | bytes 2502656 | tf_op jit(solution)/shard_map/pkgd,pktd->pkgt/dot_general | solution.py:89
  115.2 0.3 convolution_convert_fusion.2
  115.4 0.1 copy.9
  115.5 0.0 copy-done
  115.5 0.7 fusion.6
  116.2 0.4 convolution_convert_fusion.1
  116.7 0.1 reshape.67
  116.7 53.6 %all_to_all.10 = bf16[32,2,1032]{2,1,0:T(2,128)(2,1)S(1)} all-to-all(bf16[32,2,1032]{2,1,0:T(2,128)(2,1)S(1)} %reshape.67), channel_id=1, replica_groups=mesh['rep'=2,'seq'=32,'tp'=8] {'seq'}, dimensions={0} | all-to-all | bytes 264192 | tf_op jit(solution)/shard_map/all_to_all | solution.py:40
  170.3 0.1 convert_reduce_fusion.1
  170.5 0.7 fusion.43
  (5 shorter events, 0.1 us)
Async XLA Ops:
  0.0 115.5 %copy-start = (bf16[128,1,64,128]{3,2,1,0:T(8,128)(2,1)S(1)}, bf16[128,1,64,128]{3,2,1,0:T(8,128)(2,1)}, u32[]{:S(2)}) copy-start(bf16[128,1,64,128]{3,2,1,0:T(8,128)(2,1)} %param.8) | copy-start | bytes 6291460
  1.5 110.5 %all-to-all-start = ((bf16[32,2,8,128]{3,2,1,0:T(8,128)(2,1)}), bf16[32,2,8,128]{3,2,1,0:T(8,128)(2,1)S(1)}, u32[]{:S(2)}, u32[]{:S(2)}) async-start(bf16[32,2,8,128]{3,2,1,0:T(8,128)(2,1)} %broadcast_in_dim.11), calls=%async_computation | async-start | bytes 262144 | tf_op jit(solution)/shard_map/all_to_all | solution.py:17
  49.2 42.7 %copy-start.1 = (s32[64,1024]{1,0:T(8,128)S(1)}, s32[64,1024]{1,0:T(8,128)}, u32[]{:S(2)}) copy-start(s32[64,1024]{1,0:T(8,128)} %param.10) | copy-start | bytes 786436
where the time goes:
time: 171 us
  blocking collectives  53.6 us (31%)
  matrix products  47.2 us (28%)
  starting transfers between devices  45.8 us (27%)
  other arithmetic  22.7 us (13%)
  local copies, waits for them, and re-layouts  1.72 us (1%)
    all_to_all x1, blocking collectives, summed_on_arrival(): lax.all_to_all(split_up(value, dim, devices), axis, 0, 0, tiled=True)  53.6 us
    all_to_all x1, starting transfers between devices, copy_for_each(): lax.all_to_all(jnp.broadcast_to(value[None], (devices, *value.shape)), ax...  45.8 us
    dot_general x1, matrix products, body(): jnp.einsum('bsp,bs->bp', matches, fill_weight, preferred_element_type=jnp...  42.6 us
    reduce_sum x1, other arithmetic, body(): hit_table = jnp.sum(matches.astype(jnp.float32), axis=1)  19.9 us
  transfers between devices with their start and end apart: 1, of which 0 were waited for; matrix products, arithmetic and copies ran while one was open for 38% of the time, Pallas kernels for 0%

commit v1 on v0

v1 whole, which is shorter than its diff:
```python
import functools
import math

import jax
import jax.numpy as jnp
from jax import lax
from jax.experimental import pallas as pl
from jax.experimental.pallas import tpu as pltpu
from jax.sharding import PartitionSpec as P

SHIFT = 8.0
PHASE_ROWS = 128
LANES = 128
HI = 8
MESH = pl.DeviceIdType.MESH


def kernel(
    n,
    q_hbm,
    k_hbm,
    v_hbm,
    own_hbm,
    loc_hbm,
    len_ref,
    o_ref,
    q_buf,
    k_buf,
    v_buf,
    own_buf,
    loc_buf,
    q_all,
    tok_seq,
    num_out,
    tot_out,
    num_in,
    tot_in,
    load_sem,
    low_send,
    up_send,
    up2_send,
    q_recv,
    num_send,
    tot_send,
    num_recv,
    tot_recv,
    up_here,
    up2_here,
):
    z = lax.axis_index("seq")
    tp = lax.axis_index("tp")
    per, _, head_dim = q_buf.shape
    heads = q_all.shape[1] // per
    rows = per * heads
    seqs, slots = own_buf.shape
    tokens = k_buf.shape[0]
    chunk = tokens // HI
    page = k_buf.shape[0] // (HI * (LANES // HI))
    lows = LANES // HI
    devs = PHASE_ROWS // rows
    phases = n // devs

    loads = [
        pltpu.make_async_copy(src, dst, load_sem.at[i])
        for i, (src, dst) in enumerate(
            [(q_hbm, q_buf), (own_hbm, own_buf), (loc_hbm, loc_buf), (k_hbm, k_buf), (v_hbm, v_buf)]
        )
    ]
    for load in loads:
        load.start()

    barrier = pltpu.get_barrier_semaphore()

    def greet(d, carry):
        pl.semaphore_signal(barrier, inc=1, device_id={"seq": d}, device_id_type=MESH)
        return carry

    lax.fori_loop(z + 1, n, greet, 0)

    @pl.when(z >= 1)
    def _():
        pl.semaphore_wait(barrier, z)
        pl.semaphore_signal(up_here, inc=1, device_id={"seq": z - 1}, device_id_type=MESH)

    @pl.when(z >= 2)
    def _():
        pl.semaphore_signal(up2_here, inc=1, device_id={"seq": z - 2}, device_id_type=MESH)

    loads[0].wait()
    mine = jnp.zeros((per, heads, head_dim), jnp.float32)
    wide = q_buf[...].astype(jnp.float32)
    for t in range(q_buf.shape[1] // heads):
        mine = jnp.where(tp == t, wide[:, t * heads : (t + 1) * heads, :], mine)
    q_all[z] = mine.reshape(rows, head_dim).astype(jnp.bfloat16)

    def q_copy(j, d, sem):
        return pltpu.make_async_remote_copy(
            src_ref=q_all.at[j],
            dst_ref=q_all.at[j],
            send_sem=sem,
            recv_sem=q_recv.at[j],
            device_id={"seq": d},
            device_id_type=MESH,
        )

    def send_low(i, carry):
        d = z - 1 - i
        q_copy(z, d, low_send.at[d]).start()
        return carry

    lax.fori_loop(0, z, send_low, 0)

    loads[1].wait()
    loads[2].wait()
    slot = lax.broadcasted_iota(jnp.int32, (8, slots), 1)
    sub = lax.broadcasted_iota(jnp.int32, (8, slots), 0)

    def tally(g, table):
        own = own_buf[pl.ds(pl.multiple_of(g * 8, 8), 8), :]
        loc = loc_buf[pl.ds(pl.multiple_of(g * 8, 8), 8), :]
        length = jnp.zeros((8, slots), jnp.int32)
        for i in range(8):
            length = jnp.where(sub == i, len_ref[g * 8 + i], length)
        fill = jnp.clip(length - slot * page, 0, page)
        key = jnp.where((own == z) & (fill > 0), loc, -1)
        high = key >> (lows.bit_length() - 1)
        low = key & (lows - 1)
        fill_f = fill.astype(jnp.float32)
        seq_f = (g * 8 + sub).astype(jnp.float32)
        left = [jnp.where(high == h, v, 0.0) for v in (seq_f, fill_f) for h in range(HI)]
        right = [jnp.where(low == l, 1.0, 0.0) for l in range(lows)]
        left = jnp.concatenate(left, axis=0).astype(jnp.bfloat16)
        right = jnp.concatenate(right, axis=0).astype(jnp.bfloat16)
        return table + lax.dot_general(
            left, right, (((1,), (1,)), ((), ())), preferred_element_type=jnp.float32
        )

    table = lax.fori_loop(0, seqs // 8, tally, jnp.zeros((2 * HI * 8, lows * 8), jnp.float32))
    row_id = lax.broadcasted_iota(jnp.int32, table.shape, 0)
    col_id = lax.broadcasted_iota(jnp.int32, table.shape, 1)
    table = jnp.where((row_id & 7) == (col_id & 7), table, 0.0).astype(jnp.bfloat16)
    pick = (
        lax.broadcasted_iota(jnp.int32, (2 * HI, 2 * HI * 8), 1) >> 3
        == lax.broadcasted_iota(jnp.int32, (2 * HI, 2 * HI * 8), 0)
    )
    spread = (
        lax.broadcasted_iota(jnp.int32, (lows * 8, chunk), 0) >> 3
        == lax.broadcasted_iota(jnp.int32, (lows * 8, chunk), 1) // page
    )
    pick = jnp.where(pick, 1.0, 0.0).astype(jnp.bfloat16)
    spread = jnp.where(spread, 1.0, 0.0).astype(jnp.bfloat16)
    small = jnp.dot(pick, table, preferred_element_type=jnp.float32).astype(jnp.bfloat16)
    per_token = jnp.dot(small, spread, preferred_element_type=jnp.float32)
    place = (lax.broadcasted_iota(jnp.int32, (HI, chunk), 1) % page).astype(jnp.float32)
    tok_seq[...] = jnp.where(place < per_token[HI:], per_token[:HI], -1.0)

    @pl.when(z + 1 < n)
    def _():
        pl.semaphore_wait(up_here, 1)
        q_copy(z, z + 1, up_send).start()

    @pl.when(z + 2 < n)
    def _():
        pl.semaphore_wait(up2_here, 1)

        def pass_on(j, carry):
            q_copy(j, z, up_send).wait_recv()
            q_copy(j, z + 2, up2_send.at[j]).start()
            return carry

        lax.fori_loop(0, z, pass_on, 0)
        q_copy(z, z + 2, up2_send.at[z]).start()

    loads[3].wait()
    loads[4].wait()

    def num_copy(d, s):
        return pltpu.make_async_remote_copy(
            src_ref=num_out.at[d],
            dst_ref=num_in.at[s],
            send_sem=num_send.at[d],
            recv_sem=num_recv.at[s],
            device_id={"seq": d},
            device_id_type=MESH,
        )

    def tot_copy(d, s):
        return pltpu.make_async_remote_copy(
            src_ref=tot_out.at[d // devs],
            dst_ref=tot_in.at[s],
            send_sem=tot_send.at[d],
            recv_sem=tot_recv.at[s],
            device_id={"seq": d},
            device_id_type=MESH,
        )

    log2e = math.log2(math.e)
    gain, lift = log2e / math.sqrt(head_dim), SHIFT * log2e
    eye = lax.broadcasted_iota(jnp.int32, (PHASE_ROWS, LANES), 0) == lax.broadcasted_iota(
        jnp.int32, (PHASE_ROWS, LANES), 1
    )

    def phase(g, carry):
        def arrived(i, carry):
            j = g * devs + i

            @pl.when((j > z) | ((j < z) & (z + 2 >= n)))
            def _():
                q_copy(j, z, up_send).wait_recv()

            return carry

        lax.fori_loop(0, devs, arrived, 0)
        q = q_all[pl.ds(g * devs, devs)].reshape(PHASE_ROWS, head_dim)
        first = g * (devs * per)
        row_seq = (
            first + lax.broadcasted_iota(jnp.int32, (PHASE_ROWS, chunk), 0) // heads
        ).astype(jnp.float32)

        def tile(c, sums):
            num, tot = sums
            at = pl.ds(pl.multiple_of(c * chunk, chunk), chunk)
            s = lax.dot_general(
                q, k_buf[at, :], (((1,), (1,)), ((), ())), preferred_element_type=jnp.float32
            )
            w = jnp.exp2(s * gain - lift)
            w = jnp.where(tok_seq[pl.ds(c, 1), :] == row_seq, w, 0.0)
            for i in range(chunk // LANES):
                tot = tot + w[:, i * LANES : (i + 1) * LANES]
            num = num + jnp.dot(
                w.astype(jnp.bfloat16), v_buf[at, :], preferred_element_type=jnp.float32
            )
            return num, tot

        zero = jnp.zeros((PHASE_ROWS, LANES), jnp.float32)
        num, tot = lax.fori_loop(0, HI, tile, (zero, zero))
        num_out[pl.ds(g * devs, devs)] = num.astype(jnp.bfloat16).reshape(devs, rows, head_dim)
        tot = jnp.sum(tot, axis=1, keepdims=True)
        tot_out[g] = jnp.sum(jnp.where(eye, tot, 0.0), axis=0, keepdims=True)

        def give(i, carry):
            d = g * devs + i

            @pl.when(d != z)
            def _():
                num_copy(d, z).start()
                tot_copy(d, z).start()

            @pl.when(d == z)
            def _():
                num_in[z] = num_out[z]
                tot_in[z] = tot_out[g]

            return carry

        lax.fori_loop(0, devs, give, 0)
        return carry

    lax.fori_loop(0, phases, phase, 0)

    def collect(s, carry):
        @pl.when(s != z)
        def _():
            num_copy(z, s).wait_recv()
            tot_copy(z, s).wait_recv()

        return carry

    lax.fori_loop(0, n, collect, 0)
    num = jnp.sum(num_in[...].astype(jnp.float32), axis=0)
    tot = jnp.sum(tot_in[...], axis=0)
    at = lax.broadcasted_iota(jnp.int32, (rows, LANES), 0) + lax.rem(z, devs) * rows
    tot = jnp.where(lax.broadcasted_iota(jnp.int32, (rows, LANES), 1) == at, tot, 0.0)
    o_ref[...] = (num / jnp.sum(tot, axis=1, keepdims=True)).astype(jnp.bfloat16)

    def drain(d, carry):
        @pl.when(d < z)
        def _():
            q_copy(z, d, low_send.at[d]).wait_send()

        @pl.when((z + 2 < n) & (d <= z))
        def _():
            q_copy(d, z, up2_send.at[d]).wait_send()

        @pl.when(d != z)
        def _():
            num_copy(d, z).wait_send()
            tot_copy(d, z).wait_send()

        return carry

    lax.fori_loop(0, n, drain, 0)

    @pl.when(z + 1 < n)
    def _():
        q_copy(z, z, up_send).wait_send()


def body(queries, key_pages, value_pages, page_owner, page_local, seq_lengths):
    n = lax.axis_size("seq")
    per, all_heads, head_dim = queries.shape
    pool, kv, page, _ = key_pages.shape
    heads = all_heads // lax.axis_size("tp")
    rows = per * heads
    seqs, slots = page_owner.shape
    devs = PHASE_ROWS // rows
    assert kv == 1 and pool == LANES and head_dim == LANES and seqs == n * per
    tokens = pool * page
    dma = pltpu.SemaphoreType.DMA
    out = pl.pallas_call(
        functools.partial(kernel, n),
        out_shape=jax.ShapeDtypeStruct((rows, head_dim), jnp.bfloat16),
        in_specs=[pl.BlockSpec(memory_space=pl.ANY)] * 5
        + [pl.BlockSpec(memory_space=pltpu.SMEM)],
        out_specs=pl.BlockSpec(memory_space=pltpu.VMEM),
        scratch_shapes=[
            pltpu.VMEM(queries.shape, jnp.bfloat16),
            pltpu.VMEM((tokens, head_dim), jnp.bfloat16),
            pltpu.VMEM((tokens, head_dim), jnp.bfloat16),
            pltpu.VMEM((seqs, slots), jnp.int32),
            pltpu.VMEM((seqs, slots), jnp.int32),
            pltpu.VMEM((n, rows, head_dim), jnp.bfloat16),
            pltpu.VMEM((HI, tokens // HI), jnp.float32),
            pltpu.VMEM((n, rows, head_dim), jnp.bfloat16),
            pltpu.VMEM((n // devs, 1, LANES), jnp.float32),
            pltpu.VMEM((n, rows, head_dim), jnp.bfloat16),
            pltpu.VMEM((n, 1, LANES), jnp.float32),
            dma((5,)),
            dma((n,)),
            dma,
            dma((n,)),
            dma((n,)),
            dma((n,)),
            dma((n,)),
            dma((n,)),
            dma((n,)),
            pltpu.SemaphoreType.REGULAR,
            pltpu.SemaphoreType.REGULAR,
        ],
        compiler_params=pltpu.CompilerParams(collective_id=0, has_side_effects=True),
        name="paged_attention",
    )(
        queries,
        key_pages.reshape(tokens, head_dim),
        value_pages.reshape(tokens, head_dim),
        page_owner,
        page_local,
        seq_lengths,
    )
    return out.reshape(per, heads, head_dim)


def solution(mesh):
    placed = (
        P(("rep", "seq"), None, None),
        P(("rep", "seq"), "tp", None, None),
        P(("rep", "seq"), "tp", None, None),
        P("rep", None),
        P("rep", None),
        P("rep"),
    )
    return jax.shard_map(
        body, mesh=mesh, in_specs=placed, out_specs=P(("rep", "seq"), "tp", None), check_vma=False
    )
```

time: 171 us -> 114 us (0.67)
  the two profiles are of different devices: /device:TPU:46 before, /device:TPU:96 now
where the time goes in v1:
time: 114 us
  Pallas kernels  113 us (99%)
  local copies, waits for them, and re-layouts  1.28 us (1%)
    pallas_call x1, Pallas kernels, body(): pl.pallas_call(functools.partial(kernel, n), out_shape=jax.ShapeDtypeStru...  113 us

profile of v1, /device:TPU:96, one launch (start us, length us, event | category | flops | bytes accessed | tf_op | source)
XLA Modules:
  0.0 114.0 jit_solution(4502769384621927447)
XLA Ops:
  0.0 112.7 %paged_attention.1 = bf16[16,128]{1,0:T(8,128)(2,1)} custom-call(bf16[2,64,128]{2,1,0:T(8,128)(2,1)} %q_hbm.1, bf16[8192,128]{1,0:T(8,128)(2,1)} %bitcast.3, bf16[8192,128]{1,0:T(8,128)(2,1)} %bitcast.4, s32[64,1024]{1,0:T(8,128)} %own_hbm.1, s32[64,1024]{1,0:T(8,128)} %loc_hbm.1, s32[64]{0:T(128)} %len_ref.1), custom_call_target="tpu_custom_call" | custom-call | tf_op jit(solution)/shard_map/paged_attention/pallas_call | solution.py:310
  112.7 1.3 %copy.8 = bf16[2,8,128]{2,1,0:T(8,128)(2,1)} copy(bf16[2,8,128]{2,1,0:T(8,128)(2,1)} %bitcast.5) | data formatting | bytes 8192

commit v2 on v1

--- a/solution.py
+++ b/solution.py
@@ -12,6 +12,8 @@
 PHASE_ROWS = 128
 LANES = 128
 HI = 8
+DOWN = 3
+WRAP = 5
 MESH = pl.DeviceIdType.MESH
 
 
@@ -36,9 +38,12 @@
     num_in,
     tot_in,
     load_sem,
-    low_send,
+    down_first,
+    down_send,
     up_send,
     up2_send,
+    wrap_send,
+    wrap_recv,
     q_recv,
     num_send,
     tot_send,
@@ -46,9 +51,16 @@
     tot_recv,
     up_here,
     up2_here,
+    wrap_here,
 ):
     z = lax.axis_index("seq")
     tp = lax.axis_index("tp")
+    shift = jnp.where(lax.axis_index("rep") + tp == 0, 1, 0)
+    me = lax.rem(z + n - shift, n)
+
+    def at_place(p):
+        return {"seq": lax.rem(p + shift, n)}
+
     per, _, head_dim = q_buf.shape
     heads = q_all.shape[1] // per
     rows = per * heads
@@ -72,26 +84,32 @@
     barrier = pltpu.get_barrier_semaphore()
 
     def greet(d, carry):
-        pl.semaphore_signal(barrier, inc=1, device_id={"seq": d}, device_id_type=MESH)
+        pl.semaphore_signal(barrier, inc=1, device_id=at_place(d), device_id_type=MESH)
         return carry
 
-    lax.fori_loop(z + 1, n, greet, 0)
-
-    @pl.when(z >= 1)
-    def _():
-        pl.semaphore_wait(barrier, z)
-        pl.semaphore_signal(up_here, inc=1, device_id={"seq": z - 1}, device_id_type=MESH)
-
-    @pl.when(z >= 2)
-    def _():
-        pl.semaphore_signal(up2_here, inc=1, device_id={"seq": z - 2}, device_id_type=MESH)
+    lax.fori_loop(me + 1, n, greet, 0)
+
+    @pl.when(me >= 1)
+    def _():
+        pl.semaphore_wait(barrier, me)
+        pl.semaphore_signal(up_here, inc=1, device_id=at_place(me - 1), device_id_type=MESH)
+
+    @pl.when(me >= 2)
+    def _():
+        pl.semaphore_signal(up2_here, inc=1, device_id=at_place(me - 2), device_id_type=MESH)
+
+    @pl.when(me >= n - WRAP)
+    def _():
+        pl.semaphore_signal(
+            wrap_here.at[me - (n - WRAP)], inc=1, device_id=at_place(0), device_id_type=MESH
+        )
 
     loads[0].wait()
     mine = jnp.zeros((per, heads, head_dim), jnp.float32)
     wide = q_buf[...].astype(jnp.float32)
     for t in range(q_buf.shape[1] // heads):
         mine = jnp.where(tp == t, wide[:, t * heads : (t + 1) * heads, :], mine)
-    q_all[z] = mine.reshape(rows, head_dim).astype(jnp.bfloat16)
+    q_all[me] = mine.reshape(rows, head_dim).astype(jnp.bfloat16)
 
     def q_copy(j, d, sem):
         return pltpu.make_async_remote_copy(
@@ -99,16 +117,15 @@
             dst_ref=q_all.at[j],
             send_sem=sem,
             recv_sem=q_recv.at[j],
-            device_id={"seq": d},
+            device_id=at_place(d),
             device_id_type=MESH,
         )
 
-    def send_low(i, carry):
-        d = z - 1 - i
-        q_copy(z, d, low_send.at[d]).start()
-        return carry
-
-    lax.fori_loop(0, z, send_low, 0)
+    for i in range(DOWN):
+
+        @pl.when(me > i)
+        def _():
+            q_copy(me, me - 1 - i, down_first.at[i]).start()
 
     loads[1].wait()
     loads[2].wait()
@@ -154,22 +171,31 @@
     place = (lax.broadcasted_iota(jnp.int32, (HI, chunk), 1) % page).astype(jnp.float32)
     tok_seq[...] = jnp.where(place < per_token[HI:], per_token[:HI], -1.0)
 
-    @pl.when(z + 1 < n)
+    @pl.when(me + 1 < n)
     def _():
         pl.semaphore_wait(up_here, 1)
-        q_copy(z, z + 1, up_send).start()
-
-    @pl.when(z + 2 < n)
+        q_copy(me, me + 1, up_send).start()
+
+    @pl.when(me + 2 < n)
     def _():
         pl.semaphore_wait(up2_here, 1)
-
-        def pass_on(j, carry):
-            q_copy(j, z, up_send).wait_recv()
-            q_copy(j, z + 2, up2_send.at[j]).start()
-            return carry
-
-        lax.fori_loop(0, z, pass_on, 0)
-        q_copy(z, z + 2, up2_send.at[z]).start()
+        q_copy(me, me + 2, up2_send.at[me]).start()
+
+    def wrap_copy(i, p):
+        return pltpu.make_async_remote_copy(
+            src_ref=q_all.at[pl.ds(0, devs)],
+            dst_ref=q_all.at[pl.ds(0, devs)],
+            send_sem=wrap_send.at[i],
+            recv_sem=wrap_recv,
+            device_id=at_place(p),
+            device_id_type=MESH,
+        )
+
+    def goes_up(j):
+        return (j < me) & (me + 2 < n) & ((j >= devs) | (me + 2 < n - WRAP))
+
+    def goes_down(j):
+        return (j > me) & (me >= DOWN)
 
     loads[3].wait()
     loads[4].wait()
@@ -180,7 +206,7 @@
             dst_ref=num_in.at[s],
             send_sem=num_send.at[d],
             recv_sem=num_recv.at[s],
-            device_id={"seq": d},
+            device_id=at_place(d),
             device_id_type=MESH,
         )
 
@@ -190,7 +216,7 @@
             dst_ref=tot_in.at[s],
             send_sem=tot_send.at[d],
             recv_sem=tot_recv.at[s],
-            device_id={"seq": d},
+            device_id=at_place(d),
             device_id_type=MESH,
         )
 
@@ -201,21 +227,33 @@
     )
 
     def phase(g, carry):
+        @pl.when((g == 0) & (me >= n - WRAP))
+        def _():
+            wrap_copy(0, me).wait_recv()
+
         def arrived(i, carry):
             j = g * devs + i
 
-            @pl.when((j > z) | ((j < z) & (z + 2 >= n)))
+            @pl.when((j != me) & ((g > 0) | (me < n - WRAP)))
             def _():
-                q_copy(j, z, up_send).wait_recv()
+                q_copy(j, me, up_send).wait_recv()
+
+            @pl.when(goes_up(j))
+            def _():
+                q_copy(j, me + 2, up2_send.at[j]).start()
+
+            @pl.when(goes_down(j))
+            def _():
+                q_copy(j, me - DOWN, down_send.at[j]).start()
 
             return carry
 
         lax.fori_loop(0, devs, arrived, 0)
         q = q_all[pl.ds(g * devs, devs)].reshape(PHASE_ROWS, head_dim)
-        first = g * (devs * per)
-        row_seq = (
-            first + lax.broadcasted_iota(jnp.int32, (PHASE_ROWS, chunk), 0) // heads
-        ).astype(jnp.float32)
+        row = lax.broadcasted_iota(jnp.int32, (PHASE_ROWS, 1), 0)
+        source = g * devs + row // rows + shift
+        source = jnp.where(source >= n, source - n, source)
+        row_seq = (source * per + row % rows // heads).astype(jnp.float32)
 
         def tile(c, sums):
             num, tot = sums
@@ -233,7 +271,7 @@
             return num, tot
 
         zero = jnp.zeros((PHASE_ROWS, LANES), jnp.float32)
-        num, tot = lax.fori_loop(0, HI, tile, (zero, zero))
+        num, tot = lax.fori_loop(0, HI, tile, (zero, zero), unroll=2)
         num_out[pl.ds(g * devs, devs)] = num.astype(jnp.bfloat16).reshape(devs, rows, head_dim)
         tot = jnp.sum(tot, axis=1, keepdims=True)
         tot_out[g] = jnp.sum(jnp.where(eye, tot, 0.0), axis=0, keepdims=True)
@@ -241,59 +279,77 @@
         def give(i, carry):
             d = g * devs + i
 
-            @pl.when(d != z)
+            @pl.when(d != me)
             def _():
-                num_copy(d, z).start()
-                tot_copy(d, z).start()
-
-            @pl.when(d == z)
+                num_copy(d, me).start()
+                tot_copy(d, me).start()
+
+            @pl.when(d == me)
             def _():
-                num_in[z] = num_out[z]
-                tot_in[z] = tot_out[g]
+                num_in[me] = num_out[me]
+                tot_in[me] = tot_out[g]
 
             return carry
 
         lax.fori_loop(0, devs, give, 0)
+
+        @pl.when((g == 0) & (me == 0))
+        def _():
+            for i in range(WRAP):
+                pl.semaphore_wait(wrap_here.at[i], 1)
+                wrap_copy(i, n - WRAP + i).start()
+
         return carry
 
     lax.fori_loop(0, phases, phase, 0)
 
     def collect(s, carry):
-        @pl.when(s != z)
-        def _():
-            num_copy(z, s).wait_recv()
-            tot_copy(z, s).wait_recv()
+        @pl.when(s != me)
+        def _():
+            num_copy(me, s).wait_recv()
+            tot_copy(me, s).wait_recv()
 
         return carry
 
     lax.fori_loop(0, n, collect, 0)
     num = jnp.sum(num_in[...].astype(jnp.float32), axis=0)
     tot = jnp.sum(tot_in[...], axis=0)
-    at = lax.broadcasted_iota(jnp.int32, (rows, LANES), 0) + lax.rem(z, devs) * rows
+    at = lax.broadcasted_iota(jnp.int32, (rows, LANES), 0) + lax.rem(me, devs) * rows
     tot = jnp.where(lax.broadcasted_iota(jnp.int32, (rows, LANES), 1) == at, tot, 0.0)
     o_ref[...] = (num / jnp.sum(tot, axis=1, keepdims=True)).astype(jnp.bfloat16)
 
     def drain(d, carry):
-        @pl.when(d < z)
-        def _():
-            q_copy(z, d, low_send.at[d]).wait_send()
-
-        @pl.when((z + 2 < n) & (d <= z))
-        def _():
-            q_copy(d, z, up2_send.at[d]).wait_send()
-
-        @pl.when(d != z)
-        def _():
-            num_copy(d, z).wait_send()
-            tot_copy(d, z).wait_send()
+        @pl.when(goes_up(d) | ((d == me) & (me + 2 < n)))
+        def _():
+            q_copy(d, me, up2_send.at[d]).wait_send()
+
+        @pl.when(goes_down(d))
+        def _():
+            q_copy(d, me, down_send.at[d]).wait_send()
+
+        @pl.when(d != me)
+        def _():
+            num_copy(d, me).wait_send()
+            tot_copy(d, me).wait_send()
 
         return carry
 
     lax.fori_loop(0, n, drain, 0)
 
-    @pl.when(z + 1 < n)
-    def _():
-        q_copy(z, z, up_send).wait_send()
+    for i in range(DOWN):
+
+        @pl.when(me > i)
+        def _():
+            q_copy(me, me, down_first.at[i]).wait_send()
+
+    @pl.when(me + 1 < n)
+    def _():
+        q_copy(me, me, up_send).wait_send()
+
+    @pl.when(me == 0)
+    def _():
+        for i in range(WRAP):
+            wrap_copy(i, me).wait_send()
 
 
 def body(queries, key_pages, value_pages, page_owner, page_local, seq_lengths):
@@ -326,9 +382,12 @@
             pltpu.VMEM((n, rows, head_dim), jnp.bfloat16),
             pltpu.VMEM((n, 1, LANES), jnp.float32),
             dma((5,)),
+            dma((DOWN,)),
             dma((n,)),
             dma,
             dma((n,)),
+            dma((WRAP,)),
+            dma,
             dma((n,)),
             dma((n,)),
             dma((n,)),
@@ -336,6 +395,7 @@
             dma((n,)),
             pltpu.SemaphoreType.REGULAR,
             pltpu.SemaphoreType.REGULAR,
+            pltpu.SemaphoreType.REGULAR((WRAP,)),
         ],
         compiler_params=pltpu.CompilerParams(collective_id=0, has_side_effects=True),
         name="paged_attention",

time: 114 us -> 121 us (1.061)
  Pallas kernels: 113 us -> 120 us
    pallas_call x1, Pallas kernels: 113 us -> 120 us  [body(): pl.pallas_call(functools.partial(kernel, n), out_shape=jax.ShapeDtypeStru...]
where the time goes in v2:
time: 121 us
  Pallas kernels  120 us (99%)
  local copies, waits for them, and re-layouts  1.28 us (1%)
    pallas_call x1, Pallas kernels, body(): pl.pallas_call(functools.partial(kernel, n), out_shape=jax.ShapeDtypeStru...  120 us

profile of v2, /device:TPU:96, one launch (start us, length us, event | category | flops | bytes accessed | tf_op | source)
XLA Modules:
  0.0 121.2 jit_solution(18303615405654900965)
XLA Ops:
  0.0 119.9 %paged_attention.1 = bf16[16,128]{1,0:T(8,128)(2,1)} custom-call(bf16[2,64,128]{2,1,0:T(8,128)(2,1)} %q_hbm.1, bf16[8192,128]{1,0:T(8,128)(2,1)} %bitcast.3, bf16[8192,128]{1,0:T(8,128)(2,1)} %bitcast.4, s32[64,1024]{1,0:T(8,128)} %own_hbm.1, s32[64,1024]{1,0:T(8,128)} %loc_hbm.1, s32[64]{0:T(128)} %len_ref.1), custom_call_target="tpu_custom_call" | custom-call | tf_op jit(solution)/shard_map/paged_attention/pallas_call | solution.py:366
  119.9 1.3 %copy.8 = bf16[2,8,128]{2,1,0:T(8,128)(2,1)} copy(bf16[2,8,128]{2,1,0:T(8,128)(2,1)} %bitcast.5) | data formatting | bytes 8192

commit v3 on v2

--- a/solution.py
+++ b/solution.py
@@ -12,8 +12,8 @@
 PHASE_ROWS = 128
 LANES = 128
 HI = 8
-DOWN = 3
 WRAP = 5
+WRAP_PHASES = 2
 MESH = pl.DeviceIdType.MESH
 
 
@@ -38,8 +38,8 @@
     num_in,
     tot_in,
     load_sem,
-    down_first,
-    down_send,
+    low_send,
+    over_send,
     up_send,
     up2_send,
     wrap_send,
@@ -121,11 +121,20 @@
             device_id_type=MESH,
         )
 
-    for i in range(DOWN):
-
-        @pl.when(me > i)
-        def _():
-            q_copy(me, me - 1 - i, down_first.at[i]).start()
+    half = n // 2
+
+    def far(j, p):
+        return j - p > half
+
+    @pl.when(far(me, 0))
+    def _():
+        q_copy(me, 0, over_send.at[0]).start()
+
+    def send_low(d, carry):
+        q_copy(me, d, low_send.at[d]).start()
+        return carry
+
+    lax.fori_loop(jnp.maximum(me - half, 0), me, send_low, 0)
 
     loads[1].wait()
     loads[2].wait()
@@ -181,21 +190,20 @@
         pl.semaphore_wait(up2_here, 1)
         q_copy(me, me + 2, up2_send.at[me]).start()
 
-    def wrap_copy(i, p):
+    def wrap_copy(g, i, p):
         return pltpu.make_async_remote_copy(
-            src_ref=q_all.at[pl.ds(0, devs)],
-            dst_ref=q_all.at[pl.ds(0, devs)],
-            send_sem=wrap_send.at[i],
-            recv_sem=wrap_recv,
+            src_ref=q_all.at[pl.ds(g * devs, devs)],
+            dst_ref=q_all.at[pl.ds(g * devs, devs)],
+            send_sem=wrap_send.at[g, i],
+            recv_sem=wrap_recv.at[g],
             device_id=at_place(p),
             device_id_type=MESH,
         )
 
     def goes_up(j):
-        return (j < me) & (me + 2 < n) & ((j >= devs) | (me + 2 < n - WRAP))
-
-    def goes_down(j):
-        return (j > me) & (me >= DOWN)
+        return ((j < me) & (me + 2 < n) & ((j >= WRAP_PHASES * devs) | (me + 2 < n - WRAP))) | far(
+            j, me + 2
+        )
 
     loads[3].wait()
     loads[4].wait()
@@ -227,28 +235,30 @@
     )
 
     def phase(g, carry):
-        @pl.when((g == 0) & (me >= n - WRAP))
-        def _():
-            wrap_copy(0, me).wait_recv()
-
-        def arrived(i, carry):
-            j = g * devs + i
-
-            @pl.when((j != me) & ((g > 0) | (me < n - WRAP)))
+        fed = (g < WRAP_PHASES) & (me >= n - WRAP)
+
+        @pl.when(fed)
+        def _():
+            wrap_copy(g, 0, me).wait_recv()
+
+        def arrived(j, carry):
+            @pl.when((j != me) & jnp.logical_not(fed))
             def _():
                 q_copy(j, me, up_send).wait_recv()
+
+            @pl.when((me == 0) & far(j, 1))
+            def _():
+                q_copy(j, 1, over_send.at[j]).start()
 
             @pl.when(goes_up(j))
             def _():
                 q_copy(j, me + 2, up2_send.at[j]).start()
 
-            @pl.when(goes_down(j))
-            def _():
-                q_copy(j, me - DOWN, down_send.at[j]).start()
-
             return carry
 
-        lax.fori_loop(0, devs, arrived, 0)
+        start = g * devs
+        stop = jnp.where(g < phases // 2, start + devs, jnp.where(g == phases // 2, n, start))
+        lax.fori_loop(start, stop, arrived, 0)
         q = q_all[pl.ds(g * devs, devs)].reshape(PHASE_ROWS, head_dim)
         row = lax.broadcasted_iota(jnp.int32, (PHASE_ROWS, 1), 0)
         source = g * devs + row // rows + shift
@@ -293,11 +303,14 @@
 
         lax.fori_loop(0, devs, give, 0)
 
-        @pl.when((g == 0) & (me == 0))
+        @pl.when((g == WRAP_PHASES - 1) & (me == 0))
         def _():
             for i in range(WRAP):
                 pl.semaphore_wait(wrap_here.at[i], 1)
-                wrap_copy(i, n - WRAP + i).start()
+                wrap_copy(0, i, n - WRAP + i).start()
+            for w in range(1, WRAP_PHASES):
+                for i in range(WRAP):
+                    wrap_copy(w, i, n - WRAP + i).start()
 
         return carry
 
@@ -323,9 +336,13 @@
         def _():
             q_copy(d, me, up2_send.at[d]).wait_send()
 
-        @pl.when(goes_down(d))
-        def _():
-            q_copy(d, me, down_send.at[d]).wait_send()
+        @pl.when((me == 0) & far(d, 1))
+        def _():
+            q_copy(d, me, over_send.at[d]).wait_send()
+
+        @pl.when((d < me) & (d >= me - half))
+        def _():
+            q_copy(me, me, low_send.at[d]).wait_send()
 
         @pl.when(d != me)
         def _():
@@ -336,11 +353,9 @@
 
     lax.fori_loop(0, n, drain, 0)
 
-    for i in range(DOWN):
-
-        @pl.when(me > i)
-        def _():
-            q_copy(me, me, down_first.at[i]).wait_send()
+    @pl.when(far(me, 0))
+    def _():
+        q_copy(me, me, over_send.at[0]).wait_send()
 
     @pl.when(me + 1 < n)
     def _():
@@ -348,8 +363,9 @@
 
     @pl.when(me == 0)
     def _():
-        for i in range(WRAP):
-            wrap_copy(i, me).wait_send()
+        for w in range(WRAP_PHASES):
+            for i in range(WRAP):
+                wrap_copy(w, i, me).wait_send()
 
 
 def body(queries, key_pages, value_pages, page_owner, page_local, seq_lengths):
@@ -382,12 +398,12 @@
             pltpu.VMEM((n, rows, head_dim), jnp.bfloat16),
             pltpu.VMEM((n, 1, LANES), jnp.float32),
             dma((5,)),
-            dma((DOWN,)),
+            dma((n,)),
             dma((n,)),
             dma,
             dma((n,)),
-            dma((WRAP,)),
-            dma,
+            dma((WRAP_PHASES, WRAP)),
+            dma((WRAP_PHASES,)),
             dma((n,)),
             dma((n,)),
             dma((n,)),

time: 121 us -> 70 us (0.58)
  the two profiles are of different devices: /device:TPU:96 before, /device:TPU:36 now
where the time goes in v3:
time: 70 us; the launch traced here: 69.8 us
  Pallas kernels  68.6 us (98%)
  local copies, waits for them, and re-layouts  1.28 us (2%)
    pallas_call x1, Pallas kernels, body(): pl.pallas_call(functools.partial(kernel, n), out_shape=jax.ShapeDtypeStru...  68.6 us

profile of v3, /device:TPU:36, one launch (start us, length us, event | category | flops | bytes accessed | tf_op | source)
XLA Modules:
  0.0 69.8 jit_solution(6463331496566804613)
XLA Ops:
  0.0 68.6 %paged_attention.1 = bf16[16,128]{1,0:T(8,128)(2,1)} custom-call(bf16[2,64,128]{2,1,0:T(8,128)(2,1)} %q_hbm.1, bf16[8192,128]{1,0:T(8,128)(2,1)} %bitcast.3, bf16[8192,128]{1,0:T(8,128)(2,1)} %bitcast.4, s32[64,1024]{1,0:T(8,128)} %own_hbm.1, s32[64,1024]{1,0:T(8,128)} %loc_hbm.1, s32[64]{0:T(128)} %len_ref.1), custom_call_target="tpu_custom_call" | custom-call | tf_op jit(solution)/shard_map/paged_attention/pallas_call | solution.py:382
  68.6 1.3 %copy.8 = bf16[2,8,128]{2,1,0:T(8,128)(2,1)} copy(bf16[2,8,128]{2,1,0:T(8,128)(2,1)} %bitcast.5) | data formatting | bytes 8192

commit v4 on v3

--- a/solution.py
+++ b/solution.py
@@ -12,7 +12,7 @@
 PHASE_ROWS = 128
 LANES = 128
 HI = 8
-WRAP = 5
+WRAP = 8
 WRAP_PHASES = 2
 MESH = pl.DeviceIdType.MESH
 
@@ -24,13 +24,14 @@
     v_hbm,
     own_hbm,
     loc_hbm,
-    len_ref,
+    len_hbm,
     o_ref,
     q_buf,
     k_buf,
     v_buf,
     own_buf,
     loc_buf,
+    len_ref,
     q_all,
     tok_seq,
     num_out,
@@ -39,7 +40,6 @@
     tot_in,
     load_sem,
     low_send,
-    over_send,
     up_send,
     up2_send,
     wrap_send,
@@ -75,7 +75,14 @@
     loads = [
         pltpu.make_async_copy(src, dst, load_sem.at[i])
         for i, (src, dst) in enumerate(
-            [(q_hbm, q_buf), (own_hbm, own_buf), (loc_hbm, loc_buf), (k_hbm, k_buf), (v_hbm, v_buf)]
+            [
+                (q_hbm, q_buf),
+                (own_hbm, own_buf),
+                (loc_hbm, loc_buf),
+                (k_hbm, k_buf),
+                (v_hbm, v_buf),
+                (len_hbm, len_ref),
+            ]
         )
     ]
     for load in loads:
@@ -128,7 +135,7 @@
 
     @pl.when(far(me, 0))
     def _():
-        q_copy(me, 0, over_send.at[0]).start()
+        q_copy(me, 0, low_send.at[0]).start()
 
     def send_low(d, carry):
         q_copy(me, d, low_send.at[d]).start()
@@ -138,6 +145,7 @@
 
     loads[1].wait()
     loads[2].wait()
+    loads[5].wait()
     slot = lax.broadcasted_iota(jnp.int32, (8, slots), 1)
     sub = lax.broadcasted_iota(jnp.int32, (8, slots), 0)
 
@@ -212,8 +220,8 @@
         return pltpu.make_async_remote_copy(
             src_ref=num_out.at[d],
             dst_ref=num_in.at[s],
-            send_sem=num_send.at[d],
-            recv_sem=num_recv.at[s],
+            send_sem=num_send,
+            recv_sem=num_recv,
             device_id=at_place(d),
             device_id_type=MESH,
         )
@@ -222,11 +230,24 @@
         return pltpu.make_async_remote_copy(
             src_ref=tot_out.at[d // devs],
             dst_ref=tot_in.at[s],
-            send_sem=tot_send.at[d],
-            recv_sem=tot_recv.at[s],
+            send_sem=tot_send,
+            recv_sem=tot_recv,
             device_id=at_place(d),
             device_id_type=MESH,
         )
+
+    def all_copies(src, dst, send, recv):
+        return pltpu.make_async_remote_copy(
+            src_ref=src.at[pl.ds(0, n - 1)],
+            dst_ref=dst.at[pl.ds(0, n - 1)],
+            send_sem=send,
+            recv_sem=recv,
+            device_id=at_place(me),
+            device_id_type=MESH,
+        )
+
+    all_num = all_copies(num_in, num_in, num_send, num_recv)
+    all_tot = all_copies(tot_in, tot_in, tot_send, tot_recv)
 
     log2e = math.log2(math.e)
     gain, lift = log2e / math.sqrt(head_dim), SHIFT * log2e
@@ -248,7 +269,7 @@
 
             @pl.when((me == 0) & far(j, 1))
             def _():
-                q_copy(j, 1, over_send.at[j]).start()
+                q_copy(j, 1, low_send.at[j]).start()
 
             @pl.when(goes_up(j))
             def _():
@@ -259,6 +280,15 @@
         start = g * devs
         stop = jnp.where(g < phases // 2, start + devs, jnp.where(g == phases // 2, n, start))
         lax.fori_loop(start, stop, arrived, 0)
+        @pl.when((g == WRAP_PHASES - 1) & (me == 0))
+        def _():
+            for i in range(WRAP):
+                pl.semaphore_wait(wrap_here.at[i], 1)
+                wrap_copy(0, i, n - WRAP + i).start()
+            for w in range(1, WRAP_PHASES):
+                for i in range(WRAP):
+                    wrap_copy(w, i, n - WRAP + i).start()
+
         q = q_all[pl.ds(g * devs, devs)].reshape(PHASE_ROWS, head_dim)
         row = lax.broadcasted_iota(jnp.int32, (PHASE_ROWS, 1), 0)
         source = g * devs + row // rows + shift
@@ -303,28 +333,12 @@
 
         lax.fori_loop(0, devs, give, 0)
 
-        @pl.when((g == WRAP_PHASES - 1) & (me == 0))
-        def _():
-            for i in range(WRAP):
-                pl.semaphore_wait(wrap_here.at[i], 1)
-                wrap_copy(0, i, n - WRAP + i).start()
-            for w in range(1, WRAP_PHASES):
-                for i in range(WRAP):
-                    wrap_copy(w, i, n - WRAP + i).start()
-
         return carry
 
     lax.fori_loop(0, phases, phase, 0)
 
-    def collect(s, carry):
-        @pl.when(s != me)
-        def _():
-            num_copy(me, s).wait_recv()
-            tot_copy(me, s).wait_recv()
-
-        return carry
-
-    lax.fori_loop(0, n, collect, 0)
+    all_num.wait_recv()
+    all_tot.wait_recv()
     num = jnp.sum(num_in[...].astype(jnp.float32), axis=0)
     tot = jnp.sum(tot_in[...], axis=0)
     at = lax.broadcasted_iota(jnp.int32, (rows, LANES), 0) + lax.rem(me, devs) * rows
@@ -338,24 +352,21 @@
 
         @pl.when((me == 0) & far(d, 1))
         def _():
-            q_copy(d, me, over_send.at[d]).wait_send()
+            q_copy(d, me, low_send.at[d]).wait_send()
 
         @pl.when((d < me) & (d >= me - half))
         def _():
             q_copy(me, me, low_send.at[d]).wait_send()
 
-        @pl.when(d != me)
-        def _():
-            num_copy(d, me).wait_send()
-            tot_copy(d, me).wait_send()
-
         return carry
 
     lax.fori_loop(0, n, drain, 0)
+    all_num.wait_send()
+    all_tot.wait_send()
 
     @pl.when(far(me, 0))
     def _():
-        q_copy(me, me, over_send.at[0]).wait_send()
+        q_copy(me, me, low_send.at[0]).wait_send()
 
     @pl.when(me + 1 < n)
     def _():
@@ -382,8 +393,7 @@
     out = pl.pallas_call(
         functools.partial(kernel, n),
         out_shape=jax.ShapeDtypeStruct((rows, head_dim), jnp.bfloat16),
-        in_specs=[pl.BlockSpec(memory_space=pl.ANY)] * 5
-        + [pl.BlockSpec(memory_space=pltpu.SMEM)],
+        in_specs=[pl.BlockSpec(memory_space=pl.ANY)] * 6,
         out_specs=pl.BlockSpec(memory_space=pltpu.VMEM),
         scratch_shapes=[
             pltpu.VMEM(queries.shape, jnp.bfloat16),
@@ -391,24 +401,24 @@
             pltpu.VMEM((tokens, head_dim), jnp.bfloat16),
             pltpu.VMEM((seqs, slots), jnp.int32),
             pltpu.VMEM((seqs, slots), jnp.int32),
+            pltpu.SMEM((seqs,), jnp.int32),
             pltpu.VMEM((n, rows, head_dim), jnp.bfloat16),
             pltpu.VMEM((HI, tokens // HI), jnp.float32),
             pltpu.VMEM((n, rows, head_dim), jnp.bfloat16),
             pltpu.VMEM((n // devs, 1, LANES), jnp.float32),
             pltpu.VMEM((n, rows, head_dim), jnp.bfloat16),
             pltpu.VMEM((n, 1, LANES), jnp.float32),
-            dma((5,)),
-            dma((n,)),
+            dma((6,)),
             dma((n,)),
             dma,
             dma((n,)),
             dma((WRAP_PHASES, WRAP)),
             dma((WRAP_PHASES,)),
             dma((n,)),
-            dma((n,)),
-            dma((n,)),
-            dma((n,)),
-            dma((n,)),
+            dma,
+            dma,
+            dma,
+            dma,
             pltpu.SemaphoreType.REGULAR,
             pltpu.SemaphoreType.REGULAR,
             pltpu.SemaphoreType.REGULAR((WRAP,)),

time: 70 us -> 68.1 us (0.973)
  Pallas kernels: 68.6 us -> 66.7 us
    pallas_call x1, Pallas kernels: 68.6 us -> 66.7 us  [body(): pl.pallas_call(functools.partial(kernel, n), out_shape=jax.ShapeDtypeStru...]
where the time goes in v4:
time: 68.1 us; the launch traced here: 67.9 us
  Pallas kernels  66.7 us (98%)
  local copies, waits for them, and re-layouts  1.28 us (2%)
    pallas_call x1, Pallas kernels, body(): pl.pallas_call(functools.partial(kernel, n), out_shape=jax.ShapeDtypeStru...  66.7 us

profile of v4, /device:TPU:36, one launch (start us, length us, event | category | flops | bytes accessed | tf_op | source)
XLA Modules:
  0.0 67.9 jit_solution(6401637663176971128)
XLA Ops:
  0.0 66.7 %paged_attention.1 = bf16[16,128]{1,0:T(8,128)(2,1)} custom-call(bf16[2,64,128]{2,1,0:T(8,128)(2,1)} %q_hbm.1, bf16[8192,128]{1,0:T(8,128)(2,1)} %bitcast.3, bf16[8192,128]{1,0:T(8,128)(2,1)} %bitcast.4, s32[64,1024]{1,0:T(8,128)} %own_hbm.1, s32[64,1024]{1,0:T(8,128)} %loc_hbm.1, s32[64]{0:T(128)} %len_hbm.1), custom_call_target="tpu_custom_call" | custom-call | tf_op jit(solution)/shard_map/paged_attention/pallas_call | solution.py:393
  66.7 1.3 %copy.8 = bf16[2,8,128]{2,1,0:T(8,128)(2,1)} copy(bf16[2,8,128]{2,1,0:T(8,128)(2,1)} %bitcast.5) | data formatting | bytes 8192

commit v5 on v4

--- a/solution.py
+++ b/solution.py
@@ -135,10 +135,10 @@
 
     @pl.when(far(me, 0))
     def _():
-        q_copy(me, 0, low_send.at[0]).start()
+        q_copy(me, 0, low_send).start()
 
     def send_low(d, carry):
-        q_copy(me, d, low_send.at[d]).start()
+        q_copy(me, d, low_send).start()
         return carry
 
     lax.fori_loop(jnp.maximum(me - half, 0), me, send_low, 0)
@@ -196,13 +196,13 @@
     @pl.when(me + 2 < n)
     def _():
         pl.semaphore_wait(up2_here, 1)
-        q_copy(me, me + 2, up2_send.at[me]).start()
-
-    def wrap_copy(g, i, p):
+        q_copy(me, me + 2, up2_send).start()
+
+    def wrap_copy(g, p):
         return pltpu.make_async_remote_copy(
             src_ref=q_all.at[pl.ds(g * devs, devs)],
             dst_ref=q_all.at[pl.ds(g * devs, devs)],
-            send_sem=wrap_send.at[g, i],
+            send_sem=wrap_send,
             recv_sem=wrap_recv.at[g],
             device_id=at_place(p),
             device_id_type=MESH,
@@ -260,7 +260,7 @@
 
         @pl.when(fed)
         def _():
-            wrap_copy(g, 0, me).wait_recv()
+            wrap_copy(g, me).wait_recv()
 
         def arrived(j, carry):
             @pl.when((j != me) & jnp.logical_not(fed))
@@ -269,11 +269,11 @@
 
             @pl.when((me == 0) & far(j, 1))
             def _():
-                q_copy(j, 1, low_send.at[j]).start()
+                q_copy(j, 1, low_send).start()
 
             @pl.when(goes_up(j))
             def _():
-                q_copy(j, me + 2, up2_send.at[j]).start()
+                q_copy(j, me + 2, up2_send).start()
 
             return carry
 
@@ -284,10 +284,10 @@
         def _():
             for i in range(WRAP):
                 pl.semaphore_wait(wrap_here.at[i], 1)
-                wrap_copy(0, i, n - WRAP + i).start()
+                wrap_copy(0, n - WRAP + i).start()
             for w in range(1, WRAP_PHASES):
                 for i in range(WRAP):
-                    wrap_copy(w, i, n - WRAP + i).start()
+                    wrap_copy(w, n - WRAP + i).start()
 
         q = q_all[pl.ds(g * devs, devs)].reshape(PHASE_ROWS, head_dim)
         row = lax.broadcasted_iota(jnp.int32, (PHASE_ROWS, 1), 0)
@@ -311,14 +311,12 @@
             return num, tot
 
         zero = jnp.zeros((PHASE_ROWS, LANES), jnp.float32)
-        num, tot = lax.fori_loop(0, HI, tile, (zero, zero), unroll=2)
+        num, tot = lax.fori_loop(0, HI, tile, (zero, zero), unroll=HI)
         num_out[pl.ds(g * devs, devs)] = num.astype(jnp.bfloat16).reshape(devs, rows, head_dim)
         tot = jnp.sum(tot, axis=1, keepdims=True)
         tot_out[g] = jnp.sum(jnp.where(eye, tot, 0.0), axis=0, keepdims=True)
 
-        def give(i, carry):
-            d = g * devs + i
-
+        def give(d, carry):
             @pl.when(d != me)
             def _():
                 num_copy(d, me).start()
@@ -327,15 +325,53 @@
             @pl.when(d == me)
             def _():
                 num_in[me] = num_out[me]
-                tot_in[me] = tot_out[g]
+                tot_in[me] = tot_out[d // devs]
 
             return carry
 
-        lax.fori_loop(0, devs, give, 0)
+        start = jnp.where(g == 1, devs // 2, g * devs)
+        stop = jnp.where(g == 0, devs // 2, (g + 1) * devs)
+        lax.fori_loop(start, stop, give, 0)
 
         return carry
 
     lax.fori_loop(0, phases, phase, 0)
+
+    def sent(sem, count, most):
+        for k in range(1, most + 1):
+
+            @pl.when(count == k)
+            def _():
+                pltpu.make_async_remote_copy(
+                    src_ref=q_all.at[pl.ds(0, k)],
+                    dst_ref=q_all.at[pl.ds(0, k)],
+                    send_sem=sem,
+                    recv_sem=q_recv.at[0],
+                    device_id=at_place(me),
+                    device_id_type=MESH,
+                ).wait_send()
+
+    low = jnp.minimum(me, half) + jnp.where(far(me, 0), 1, 0)
+    sent(low_send, jnp.where(me == 0, n - half - 2, low), half + 1)
+    below = jnp.where(me + 2 < n - WRAP, me, jnp.maximum(me - WRAP_PHASES * devs, 0))
+    up2 = jnp.where(me + 2 < n, below + 1, 0) + jnp.maximum(n - 3 - me - half, 0)
+    sent(up2_send, up2, n)
+
+    @pl.when(me + 1 < n)
+    def _():
+        q_copy(me, me, up_send).wait_send()
+
+    @pl.when(me == 0)
+    def _():
+        fed_rows = WRAP_PHASES * WRAP * devs * rows
+        pltpu.make_async_remote_copy(
+            src_ref=k_buf.at[pl.ds(0, fed_rows)],
+            dst_ref=k_buf.at[pl.ds(0, fed_rows)],
+            send_sem=wrap_send,
+            recv_sem=q_recv.at[0],
+            device_id=at_place(me),
+            device_id_type=MESH,
+        ).wait_send()
 
     all_num.wait_recv()
     all_tot.wait_recv()
@@ -344,39 +380,8 @@
     at = lax.broadcasted_iota(jnp.int32, (rows, LANES), 0) + lax.rem(me, devs) * rows
     tot = jnp.where(lax.broadcasted_iota(jnp.int32, (rows, LANES), 1) == at, tot, 0.0)
     o_ref[...] = (num / jnp.sum(tot, axis=1, keepdims=True)).astype(jnp.bfloat16)
-
-    def drain(d, carry):
-        @pl.when(goes_up(d) | ((d == me) & (me + 2 < n)))
-        def _():
-            q_copy(d, me, up2_send.at[d]).wait_send()
-
-        @pl.when((me == 0) & far(d, 1))
-        def _():
-            q_copy(d, me, low_send.at[d]).wait_send()
-
-        @pl.when((d < me) & (d >= me - half))
-        def _():
-            q_copy(me, me, low_send.at[d]).wait_send()
-
-        return carry
-
-    lax.fori_loop(0, n, drain, 0)
     all_num.wait_send()
     all_tot.wait_send()
-
-    @pl.when(far(me, 0))
-    def _():
-        q_copy(me, me, low_send.at[0]).wait_send()
-
-    @pl.when(me + 1 < n)
-    def _():
-        q_copy(me, me, up_send).wait_send()
-
-    @pl.when(me == 0)
-    def _():
-        for w in range(WRAP_PHASES):
-            for i in range(WRAP):
-                wrap_copy(w, i, me).wait_send()
 
 
 def body(queries, key_pages, value_pages, page_owner, page_local, seq_lengths):
@@ -392,7 +397,7 @@
     dma = pltpu.SemaphoreType.DMA
     out = pl.pallas_call(
         functools.partial(kernel, n),
-        out_shape=jax.ShapeDtypeStruct((rows, head_dim), jnp.bfloat16),
+        out_shape=pltpu.VMEM((rows, head_dim), jnp.bfloat16),
         in_specs=[pl.BlockSpec(memory_space=pl.ANY)] * 6,
         out_specs=pl.BlockSpec(memory_space=pltpu.VMEM),
         scratch_shapes=[
@@ -409,10 +414,10 @@
             pltpu.VMEM((n, rows, head_dim), jnp.bfloat16),
             pltpu.VMEM((n, 1, LANES), jnp.float32),
             dma((6,)),
-            dma((n,)),
-            dma,
-            dma((n,)),
-            dma((WRAP_PHASES, WRAP)),
+            dma,
+            dma,
+            dma,
+            dma,
             dma((WRAP_PHASES,)),
             dma((n,)),
             dma,

time: 68.1 us -> 63 us (0.925)
  the two profiles are of different devices: /device:TPU:36 before, /device:TPU:289 now
where the time goes in v5:
time: 63 us; the launch traced here: 62.9 us
  Pallas kernels  62.2 us (99%)
    pallas_call x1, Pallas kernels, body(): pl.pallas_call(functools.partial(kernel, n), out_shape=pltpu.VMEM((rows,...  62.2 us

profile of v5, /device:TPU:289, one launch (start us, length us, event | category | flops | bytes accessed | tf_op | source)
XLA Modules:
  0.0 62.9 jit_solution(17185436381262936668)
XLA Ops:
  0.0 62.2 %paged_attention.1 = bf16[16,128]{1,0:T(8,128)(2,1)S(1)} custom-call(bf16[2,64,128]{2,1,0:T(8,128)(2,1)} %q_hbm.1, bf16[8192,128]{1,0:T(8,128)(2,1)} %bitcast.4, bf16[8192,128]{1,0:T(8,128)(2,1)} %bitcast.5, s32[64,1024]{1,0:T(8,128)} %own_hbm.1, s32[64,1024]{1,0:T(8,128)} %loc_hbm.1, s32[64]{0:T(128)} %len_hbm.1), custom_call_target="tpu_custom_call" | custom-call | tf_op jit(solution)/shard_map/paged_attention/pallas_call | solution.py:398
  62.3 0.6 copy.8

commit v6 on v5

--- a/solution.py
+++ b/solution.py
@@ -12,7 +12,8 @@
 PHASE_ROWS = 128
 LANES = 128
 HI = 8
-WRAP = 8
+WRAP = 6
+HOP = 4
 WRAP_PHASES = 2
 MESH = pl.DeviceIdType.MESH
 
@@ -42,6 +43,7 @@
     low_send,
     up_send,
     up2_send,
+    hop_send,
     wrap_send,
     wrap_recv,
     q_recv,
@@ -51,6 +53,7 @@
     tot_recv,
     up_here,
     up2_here,
+    hop_here,
     wrap_here,
 ):
     z = lax.axis_index("seq")
@@ -105,6 +108,13 @@
     def _():
         pl.semaphore_signal(up2_here, inc=1, device_id=at_place(me - 2), device_id_type=MESH)
 
+    half = n // 2
+    first_hop = min(half + HOP, n - WRAP)
+
+    @pl.when((me >= first_hop) & (me < n - WRAP))
+    def _():
+        pl.semaphore_signal(hop_here, inc=1, device_id=at_place(me - HOP), device_id_type=MESH)
+
     @pl.when(me >= n - WRAP)
     def _():
         pl.semaphore_signal(
@@ -127,8 +137,6 @@
             device_id=at_place(d),
             device_id_type=MESH,
         )
-
-    half = n // 2
 
     def far(j, p):
         return j - p > half
@@ -208,10 +216,21 @@
             device_id_type=MESH,
         )
 
+    def hop_copy(p):
+        return pltpu.make_async_remote_copy(
+            src_ref=q_all.at[pl.ds(0, devs)],
+            dst_ref=q_all.at[pl.ds(0, devs)],
+            send_sem=hop_send,
+            recv_sem=wrap_recv.at[0],
+            device_id=at_place(p),
+            device_id_type=MESH,
+        )
+
     def goes_up(j):
-        return ((j < me) & (me + 2 < n) & ((j >= WRAP_PHASES * devs) | (me + 2 < n - WRAP))) | far(
-            j, me + 2
-        )
+        limit = jnp.where(j < devs, first_hop, jnp.where(j < WRAP_PHASES * devs, n - WRAP, n))
+        return ((j < me) & (me + 2 < limit)) | far(j, me + 2)
+
+    hops = (me + HOP >= first_hop) & (me + HOP < n - WRAP)
 
     loads[3].wait()
     loads[4].wait()
@@ -255,8 +274,21 @@
         jnp.int32, (PHASE_ROWS, LANES), 1
     )
 
+    def give(d, carry):
+        @pl.when(d != me)
+        def _():
+            num_copy(d, me).start()
+            tot_copy(d, me).start()
+
+        @pl.when(d == me)
+        def _():
+            num_in[me] = num_out[me]
+            tot_in[me] = tot_out[d // devs]
+
+        return carry
+
     def phase(g, carry):
-        fed = (g < WRAP_PHASES) & (me >= n - WRAP)
+        fed = ((g == 0) & (me >= first_hop)) | ((g < WRAP_PHASES) & (me >= n - WRAP))
 
         @pl.when(fed)
         def _():
@@ -280,6 +312,11 @@
         start = g * devs
         stop = jnp.where(g < phases // 2, start + devs, jnp.where(g == phases // 2, n, start))
         lax.fori_loop(start, stop, arrived, 0)
+        @pl.when((g == 0) & hops)
+        def _():
+            pl.semaphore_wait(hop_here, 1)
+            hop_copy(me + HOP).start()
+
         @pl.when((g == WRAP_PHASES - 1) & (me == 0))
         def _():
             for i in range(WRAP):
@@ -288,6 +325,10 @@
             for w in range(1, WRAP_PHASES):
                 for i in range(WRAP):
                     wrap_copy(w, n - WRAP + i).start()
+
+        @pl.when(g == 1)
+        def _():
+            lax.fori_loop(devs // 2, devs, give, 0)
 
         q = q_all[pl.ds(g * devs, devs)].reshape(PHASE_ROWS, head_dim)
         row = lax.broadcasted_iota(jnp.int32, (PHASE_ROWS, 1), 0)
@@ -316,23 +357,8 @@
         tot = jnp.sum(tot, axis=1, keepdims=True)
         tot_out[g] = jnp.sum(jnp.where(eye, tot, 0.0), axis=0, keepdims=True)
 
-        def give(d, carry):
-            @pl.when(d != me)
-            def _():
-                num_copy(d, me).start()
-                tot_copy(d, me).start()
-
-            @pl.when(d == me)
-            def _():
-                num_in[me] = num_out[me]
-                tot_in[me] = tot_out[d // devs]
-
-            return carry
-
-        start = jnp.where(g == 1, devs // 2, g * devs)
         stop = jnp.where(g == 0, devs // 2, (g + 1) * devs)
-        lax.fori_loop(start, stop, give, 0)
-
+        lax.fori_loop(g * devs, stop, give, 0)
         return carry
 
     lax.fori_loop(0, phases, phase, 0)
@@ -353,13 +379,18 @@
 
     low = jnp.minimum(me, half) + jnp.where(far(me, 0), 1, 0)
     sent(low_send, jnp.where(me == 0, n - half - 2, low), half + 1)
-    below = jnp.where(me + 2 < n - WRAP, me, jnp.maximum(me - WRAP_PHASES * devs, 0))
+    below = jnp.where(me + 2 < n - WRAP, me - devs, jnp.maximum(me - WRAP_PHASES * devs, 0))
+    below = jnp.where(me + 2 < first_hop, me, below)
     up2 = jnp.where(me + 2 < n, below + 1, 0) + jnp.maximum(n - 3 - me - half, 0)
     sent(up2_send, up2, n)
 
     @pl.when(me + 1 < n)
     def _():
         q_copy(me, me, up_send).wait_send()
+
+    @pl.when(hops)
+    def _():
+        hop_copy(me).wait_send()
 
     @pl.when(me == 0)
     def _():
@@ -418,12 +449,14 @@
             dma,
             dma,
             dma,
+            dma,
             dma((WRAP_PHASES,)),
             dma((n,)),
             dma,
             dma,
             dma,
             dma,
+            pltpu.SemaphoreType.REGULAR,
             pltpu.SemaphoreType.REGULAR,
             pltpu.SemaphoreType.REGULAR,
             pltpu.SemaphoreType.REGULAR((WRAP,)),

time: 63 us -> 65.7 us (1.043)
  the two profiles are of different devices: /device:TPU:289 before, /device:TPU:42 now
where the time goes in v6:
time: 65.7 us; the launch traced here: 65.5 us
  Pallas kernels  64.9 us (99%)
    pallas_call x1, Pallas kernels, body(): pl.pallas_call(functools.partial(kernel, n), out_shape=pltpu.VMEM((rows,...  64.9 us

profile of v6, /device:TPU:42, one launch (start us, length us, event | category | flops | bytes accessed | tf_op | source)
XLA Modules:
  0.0 65.5 jit_solution(10342637090886622295)
XLA Ops:
  0.0 64.9 %paged_attention.1 = bf16[16,128]{1,0:T(8,128)(2,1)S(1)} custom-call(bf16[2,64,128]{2,1,0:T(8,128)(2,1)} %q_hbm.1, bf16[8192,128]{1,0:T(8,128)(2,1)} %bitcast.4, bf16[8192,128]{1,0:T(8,128)(2,1)} %bitcast.5, s32[64,1024]{1,0:T(8,128)} %own_hbm.1, s32[64,1024]{1,0:T(8,128)} %loc_hbm.1, s32[64]{0:T(128)} %len_hbm.1), custom_call_target="tpu_custom_call" | custom-call | tf_op jit(solution)/shard_map/paged_attention/pallas_call | solution.py:429
  64.9 0.6 copy.8

commit v7 on v6

--- a/solution.py
+++ b/solution.py
@@ -326,10 +326,6 @@
                 for i in range(WRAP):
                     wrap_copy(w, n - WRAP + i).start()
 
-        @pl.when(g == 1)
-        def _():
-            lax.fori_loop(devs // 2, devs, give, 0)
-
         q = q_all[pl.ds(g * devs, devs)].reshape(PHASE_ROWS, head_dim)
         row = lax.broadcasted_iota(jnp.int32, (PHASE_ROWS, 1), 0)
         source = g * devs + row // rows + shift
@@ -357,8 +353,9 @@
         tot = jnp.sum(tot, axis=1, keepdims=True)
         tot_out[g] = jnp.sum(jnp.where(eye, tot, 0.0), axis=0, keepdims=True)
 
+        start = jnp.where(g == 1, devs // 2, g * devs)
         stop = jnp.where(g == 0, devs // 2, (g + 1) * devs)
-        lax.fori_loop(g * devs, stop, give, 0)
+        lax.fori_loop(start, stop, give, 0)
         return carry
 
     lax.fori_loop(0, phases, phase, 0)

time: 65.7 us -> 62.6 us (0.953)
  the two profiles are of different devices: /device:TPU:42 before, /device:TPU:172 now
where the time goes in v7:
time: 62.6 us; the launch traced here: 62.5 us
  Pallas kernels  61.9 us (99%)
    pallas_call x1, Pallas kernels, body(): pl.pallas_call(functools.partial(kernel, n), out_shape=pltpu.VMEM((rows,...  61.9 us

profile of v7, /device:TPU:172, one launch (start us, length us, event | category | flops | bytes accessed | tf_op | source)
XLA Modules:
  0.0 62.5 jit_solution(8322253574461868481)
XLA Ops:
  0.0 61.9 %paged_attention.1 = bf16[16,128]{1,0:T(8,128)(2,1)S(1)} custom-call(bf16[2,64,128]{2,1,0:T(8,128)(2,1)} %q_hbm.1, bf16[8192,128]{1,0:T(8,128)(2,1)} %bitcast.4, bf16[8192,128]{1,0:T(8,128)(2,1)} %bitcast.5, s32[64,1024]{1,0:T(8,128)} %own_hbm.1, s32[64,1024]{1,0:T(8,128)} %loc_hbm.1, s32[64]{0:T(128)} %len_hbm.1), custom_call_target="tpu_custom_call" | custom-call | tf_op jit(solution)/shard_map/paged_attention/pallas_call | solution.py:426
  61.9 0.6 copy.8

commit v8 on v7

--- a/solution.py
+++ b/solution.py
@@ -353,8 +353,9 @@
         tot = jnp.sum(tot, axis=1, keepdims=True)
         tot_out[g] = jnp.sum(jnp.where(eye, tot, 0.0), axis=0, keepdims=True)
 
-        start = jnp.where(g == 1, devs // 2, g * devs)
-        stop = jnp.where(g == 0, devs // 2, (g + 1) * devs)
+        late = me >= n - WRAP
+        start = jnp.where(late & (g == 1), devs // 2, g * devs)
+        stop = jnp.where(late & (g == 0), devs // 2, (g + 1) * devs)
         lax.fori_loop(start, stop, give, 0)
         return carry
 

time: 62.6 us -> 63.8 us (1.019)
  the two profiles are of different devices: /device:TPU:172 before, /device:TPU:108 now
where the time goes in v8:
time: 63.8 us; the launch traced here: 63.7 us
  Pallas kernels  63.1 us (99%)
    pallas_call x1, Pallas kernels, body(): pl.pallas_call(functools.partial(kernel, n), out_shape=pltpu.VMEM((rows,...  63.1 us

profile of v8, /device:TPU:108, one launch (start us, length us, event | category | flops | bytes accessed | tf_op | source)
XLA Modules:
  0.0 63.7 jit_solution(16283189740983172391)
XLA Ops:
  0.0 63.1 %paged_attention.1 = bf16[16,128]{1,0:T(8,128)(2,1)S(1)} custom-call(bf16[2,64,128]{2,1,0:T(8,128)(2,1)} %q_hbm.1, bf16[8192,128]{1,0:T(8,128)(2,1)} %bitcast.4, bf16[8192,128]{1,0:T(8,128)(2,1)} %bitcast.5, s32[64,1024]{1,0:T(8,128)} %own_hbm.1, s32[64,1024]{1,0:T(8,128)} %loc_hbm.1, s32[64]{0:T(128)} %len_hbm.1), custom_call_target="tpu_custom_call" | custom-call | tf_op jit(solution)/shard_map/paged_attention/pallas_call | solution.py:427
  63.1 0.6 copy.8

commit v9 on v7

--- a/solution.py
+++ b/solution.py
@@ -353,8 +353,9 @@
         tot = jnp.sum(tot, axis=1, keepdims=True)
         tot_out[g] = jnp.sum(jnp.where(eye, tot, 0.0), axis=0, keepdims=True)
 
-        start = jnp.where(g == 1, devs // 2, g * devs)
-        stop = jnp.where(g == 0, devs // 2, (g + 1) * devs)
+        at_once = devs * 5 // 8
+        start = jnp.where(g == 1, at_once, g * devs)
+        stop = jnp.where(g == 0, at_once, (g + 1) * devs)
         lax.fori_loop(start, stop, give, 0)
         return carry
 

time: 62.6 us -> 64.3 us (1.027)
  the two profiles are of different devices: /device:TPU:172 before, /device:TPU:44 now
where the time goes in v9:
time: 64.3 us; the launch traced here: 64.2 us
  Pallas kernels  63.6 us (99%)
    pallas_call x1, Pallas kernels, body(): pl.pallas_call(functools.partial(kernel, n), out_shape=pltpu.VMEM((rows,...  63.6 us

profile of v9, /device:TPU:44, one launch (start us, length us, event | category | flops | bytes accessed | tf_op | source)
XLA Modules:
  0.0 64.2 jit_solution(3939523512034761729)
XLA Ops:
  0.0 63.6 %paged_attention.1 = bf16[16,128]{1,0:T(8,128)(2,1)S(1)} custom-call(bf16[2,64,128]{2,1,0:T(8,128)(2,1)} %q_hbm.1, bf16[8192,128]{1,0:T(8,128)(2,1)} %bitcast.4, bf16[8192,128]{1,0:T(8,128)(2,1)} %bitcast.5, s32[64,1024]{1,0:T(8,128)} %own_hbm.1, s32[64,1024]{1,0:T(8,128)} %loc_hbm.1, s32[64]{0:T(128)} %len_hbm.1), custom_call_target="tpu_custom_call" | custom-call | tf_op jit(solution)/shard_map/paged_attention/pallas_call | solution.py:427
  63.6 0.6 copy.8

commit v10 on v7

--- a/solution.py
+++ b/solution.py
@@ -353,8 +353,9 @@
         tot = jnp.sum(tot, axis=1, keepdims=True)
         tot_out[g] = jnp.sum(jnp.where(eye, tot, 0.0), axis=0, keepdims=True)
 
-        start = jnp.where(g == 1, devs // 2, g * devs)
-        stop = jnp.where(g == 0, devs // 2, (g + 1) * devs)
+        holds = (me < n - WRAP - 2) | (me >= n - WRAP)
+        start = jnp.where(holds & (g == 1), devs // 2, g * devs)
+        stop = jnp.where(holds & (g == 0), devs // 2, (g + 1) * devs)
         lax.fori_loop(start, stop, give, 0)
         return carry
 

time: 62.6 us -> 64.1 us (1.024)
  the two profiles are of different devices: /device:TPU:172 before, /device:TPU:108 now
where the time goes in v10:
time: 64.1 us; the launch traced here: 64 us
  Pallas kernels  63.4 us (99%)
    pallas_call x1, Pallas kernels, body(): pl.pallas_call(functools.partial(kernel, n), out_shape=pltpu.VMEM((rows,...  63.4 us

profile of v10, /device:TPU:108, one launch (start us, length us, event | category | flops | bytes accessed | tf_op | source)
XLA Modules:
  0.0 64.0 jit_solution(8439220518192036713)
XLA Ops:
  0.0 63.4 %paged_attention.1 = bf16[16,128]{1,0:T(8,128)(2,1)S(1)} custom-call(bf16[2,64,128]{2,1,0:T(8,128)(2,1)} %q_hbm.1, bf16[8192,128]{1,0:T(8,128)(2,1)} %bitcast.4, bf16[8192,128]{1,0:T(8,128)(2,1)} %bitcast.5, s32[64,1024]{1,0:T(8,128)} %own_hbm.1, s32[64,1024]{1,0:T(8,128)} %loc_hbm.1, s32[64]{0:T(128)} %len_hbm.1), custom_call_target="tpu_custom_call" | custom-call | tf_op jit(solution)/shard_map/paged_attention/pallas_call | solution.py:427
  63.4 0.6 copy.8
